TPU v7x, 16 devices: a whole 2x2x2 slice. The times are simulated.
16 devices in a mesh: dp: 16 (over z, y, x, core).
Axes of the slice: x: 2, y: 2, z: 2, core: 2. Of those that a mesh axis runs over, the one named last changes fastest.
Arguments:
- img_emb: bfloat16 [32768, 768], P('dp')
- txt_emb: bfloat16 [32768, 768], P('dp')
- log_temp: float32 [1], replicated
- logit_bias: float32 [1], replicated
Outputs:
- output 1: float32 [1], replicated
- output 2: float32 [32768, 768], P('dp')
- output 3: float32 [32768, 768], P('dp')
- output 4: float32 [1], replicated
- output 5: float32 [1], replicated
All inputs are finite; a program needn't handle non-finite values.
Results may differ from a plain program's by a relative error of at most 0.001.
Values are sent between devices in bfloat16 or wider.
A program may use at most 1 GiB of HBM per device.

v0:
```python
import jax
import jax.numpy as jnp
from jax import lax
from jax.sharding import PartitionSpec as P


def block_terms(img_local, txt_block, labels, temp_scale, bias_val):
    dot_vals = jnp.einsum('id,jd->ij', img_local, txt_block, preferred_element_type=jnp.float32)
    margin = labels * (temp_scale * dot_vals + bias_val)
    loss_part = jnp.sum(jax.nn.softplus(-margin))
    grad_coef = -labels * jax.nn.sigmoid(-margin)
    coef_bf16 = grad_coef.astype(jnp.bfloat16)
    img_part = jnp.einsum('ij,jd->id', coef_bf16, txt_block, preferred_element_type=jnp.float32)
    txt_part = jnp.einsum('ij,id->jd', coef_bf16, img_local, preferred_element_type=jnp.float32)
    return loss_part, jnp.sum(grad_coef), jnp.sum(grad_coef * dot_vals), img_part, txt_part


def solution(mesh):
    axis_name = mesh.axis_names[0]
    n_dev = mesh.shape[axis_name]
    shift_pairs = [(source, (source - 1) % n_dev) for source in range(n_dev)]

    def per_device(img_local, txt_local, log_temp, logit_bias):
        local_rows = img_local.shape[0]
        n_total = local_rows * n_dev
        temp_scale = jnp.exp(log_temp[0])
        bias_val = logit_bias[0]
        row_ids = jnp.arange(local_rows)
        diag_labels = jnp.where(row_ids[:, None] == row_ids[None, :], 1.0, -1.0)
        first_terms = block_terms(img_local, txt_local, diag_labels, temp_scale, bias_val)

        def step_fn(step_idx, loop_state):
            txt_block, txt_acc, loss_acc, bias_acc, temp_acc, img_acc = loop_state
            txt_block = lax.ppermute(txt_block, axis_name, shift_pairs)
            txt_acc = lax.ppermute(txt_acc, axis_name, shift_pairs)
            loss_part, bias_part, temp_part, img_part, txt_part = block_terms(img_local, txt_block, -1.0, temp_scale, bias_val)
            return (txt_block, txt_acc + txt_part, loss_acc + loss_part, bias_acc + bias_part, temp_acc + temp_part, img_acc + img_part)

        init_state = (txt_local, first_terms[4], first_terms[0], first_terms[1], first_terms[2], first_terms[3])
        final_state = lax.fori_loop(1, n_dev, step_fn, init_state)
        txt_acc = lax.ppermute(final_state[1], axis_name, shift_pairs)
        global_sums = lax.psum(jnp.stack([final_state[2], final_state[3], final_state[4]]), axis_name)
        factor = temp_scale / n_total
        return (global_sums[0:1] / n_total, final_state[5] * factor, txt_acc * factor, global_sums[2:3] * factor, global_sums[1:2] / n_total)

    return jax.shard_map(per_device, mesh=mesh, in_specs=(P(axis_name, None), P(axis_name, None), P(None), P(None)), out_specs=(P(None), P(axis_name, None), P(axis_name, None), P(None), P(None)), check_vma=False)
```

profile of v0, /device:TPU:0, one launch (start us, length us, event | category | flops | bytes accessed | tf_op | source)
XLA Modules:
  0.0 1999.0 jit_solution(14080574517050922838)
XLA Ops:
  3.9 24.8 %multiply_reduce_fusion.1 = (f32[]{:T(128)}, f32[]{:T(128)}, f32[]{:T(128)}, bf16[2048,2048]{1,0:T(8,128)(2,1)S(1)}) fusion(f32[]{:T(128)} %bitcast.24, f32[]{:T(128)} %bitcast, bf16[2048,768]{1,0:T(8,128)(2,1)} %param.6, bf16[2048,768]{1,0:T(8,128)(2,1)S(1)} %copy.34), kind=kOutput, calls=%fused_computation.17 | convolution fusion | flops 6530531328 | bytes 14680084 | tf_op jit(solution)/shard_map/id,jd->ij/dot_general | solution.py:8
  46.2 1835.9 %while.20 = (s32[]{:T(128)}, bf16[2048,768]{1,0:T(8,128)(2,1)}, f32[2048,768]{1,0:T(8,128)}, f32[]{:T(128)}, f32[]{:T(128)}, /*index=5*/f32[]{:T(128)}, f32[2048...) while((s32[]{:T(128)}, bf16[2048,768]{1,0:T(8,128)(2,1)}, ...), condition=%wide.region_7.8_spmd, body=%wide.region_3.7_spmd.sunk | while | flops 19447939072 | bytes 144703792 | solution.py:40
  51.5 34.1 %collective-permute-done = bf16[2048,768]{1,0:T(8,128)(2,1)S(1)} collective-permute-done((bf16[2048,768]{1,0:T(8,128)(2,1)}, bf16[2048,768]{1,0:T(8,128)(2,1)S(1)}, u32[]{:S(2)}, u32[]{:S(2)}) %collective-permute-start) | collective-permute-done | bytes 3145760 | tf_op jit(solution)/shard_map/while/body/eval_jaxpr/ppermute | solution.py:34
  173.2 34.7 %collective-permute-done = bf16[2048,768]{1,0:T(8,128)(2,1)S(1)} collective-permute-done((bf16[2048,768]{1,0:T(8,128)(2,1)}, bf16[2048,768]{1,0:T(8,128)(2,1)S(1)}, u32[]{:S(2)}, u32[]{:S(2)}) %collective-permute-start) | collective-permute-done | bytes 3145760 | tf_op jit(solution)/shard_map/while/body/eval_jaxpr/ppermute | solution.py:34
  208.0 24.0 %multiply_reduce_fusion.3 = (f32[]{:T(128)}, f32[]{:T(128)}, f32[]{:T(128)}, f32[2048,2048]{1,0:T(8,128)}) fusion(f32[]{:T(128)} %get-tuple-element.201, f32[]{:T(128)} %get-tuple-element.199, bf16[2048,768]{1,0:T(8,128)(2,1)} %get-tuple-element.200, bf16[2048,768]{1,0:T(8,128)(2,1)S(1)} %collective-permute-done), kind=kOutput, calls=%fused_computation.2.clone.1 | convolution fusion | flops 6509559808 | bytes 23068692 | tf_op jit(solution)/shard_map/while/body/eval_jaxpr/id,jd->ij/dot_general | solution.py:8
  295.6 34.7 %collective-permute-done = bf16[2048,768]{1,0:T(8,128)(2,1)S(1)} collective-permute-done((bf16[2048,768]{1,0:T(8,128)(2,1)}, bf16[2048,768]{1,0:T(8,128)(2,1)S(1)}, u32[]{:S(2)}, u32[]{:S(2)}) %collective-permute-start) | collective-permute-done | bytes 3145760 | tf_op jit(solution)/shard_map/while/body/eval_jaxpr/ppermute | solution.py:34
  417.9 34.7 %collective-permute-done = bf16[2048,768]{1,0:T(8,128)(2,1)S(1)} collective-permute-done((bf16[2048,768]{1,0:T(8,128)(2,1)}, bf16[2048,768]{1,0:T(8,128)(2,1)S(1)}, u32[]{:S(2)}, u32[]{:S(2)}) %collective-permute-start) | collective-permute-done | bytes 3145760 | tf_op jit(solution)/shard_map/while/body/eval_jaxpr/ppermute | solution.py:34
  452.6 24.0 %multiply_reduce_fusion.3 = (f32[]{:T(128)}, f32[]{:T(128)}, f32[]{:T(128)}, f32[2048,2048]{1,0:T(8,128)}) fusion(f32[]{:T(128)} %get-tuple-element.201, f32[]{:T(128)} %get-tuple-element.199, bf16[2048,768]{1,0:T(8,128)(2,1)} %get-tuple-element.200, bf16[2048,768]{1,0:T(8,128)(2,1)S(1)} %collective-permute-done), kind=kOutput, calls=%fused_computation.2.clone.1 | convolution fusion | flops 6509559808 | bytes 23068692 | tf_op jit(solution)/shard_map/while/body/eval_jaxpr/id,jd->ij/dot_general | solution.py:8
  540.2 34.7 %collective-permute-done = bf16[2048,768]{1,0:T(8,128)(2,1)S(1)} collective-permute-done((bf16[2048,768]{1,0:T(8,128)(2,1)}, bf16[2048,768]{1,0:T(8,128)(2,1)S(1)}, u32[]{:S(2)}, u32[]{:S(2)}) %collective-permute-start) | collective-permute-done | bytes 3145760 | tf_op jit(solution)/shard_map/while/body/eval_jaxpr/ppermute | solution.py:34
  662.6 34.7 %collective-permute-done = bf16[2048,768]{1,0:T(8,128)(2,1)S(1)} collective-permute-done((bf16[2048,768]{1,0:T(8,128)(2,1)}, bf16[2048,768]{1,0:T(8,128)(2,1)S(1)}, u32[]{:S(2)}, u32[]{:S(2)}) %collective-permute-start) | collective-permute-done | bytes 3145760 | tf_op jit(solution)/shard_map/while/body/eval_jaxpr/ppermute | solution.py:34
  697.3 24.0 %multiply_reduce_fusion.3 = (f32[]{:T(128)}, f32[]{:T(128)}, f32[]{:T(128)}, f32[2048,2048]{1,0:T(8,128)}) fusion(f32[]{:T(128)} %get-tuple-element.201, f32[]{:T(128)} %get-tuple-element.199, bf16[2048,768]{1,0:T(8,128)(2,1)} %get-tuple-element.200, bf16[2048,768]{1,0:T(8,128)(2,1)S(1)} %collective-permute-done), kind=kOutput, calls=%fused_computation.2.clone.1 | convolution fusion | flops 6509559808 | bytes 23068692 | tf_op jit(solution)/shard_map/while/body/eval_jaxpr/id,jd->ij/dot_general | solution.py:8
  784.9 34.7 %collective-permute-done = bf16[2048,768]{1,0:T(8,128)(2,1)S(1)} collective-permute-done((bf16[2048,768]{1,0:T(8,128)(2,1)}, bf16[2048,768]{1,0:T(8,128)(2,1)S(1)}, u32[]{:S(2)}, u32[]{:S(2)}) %collective-permute-start) | collective-permute-done | bytes 3145760 | tf_op jit(solution)/shard_map/while/body/eval_jaxpr/ppermute | solution.py:34
  819.6 24.0 %multiply_reduce_fusion.3 = (f32[]{:T(128)}, f32[]{:T(128)}, f32[]{:T(128)}, f32[2048,2048]{1,0:T(8,128)}) fusion(f32[]{:T(128)} %get-tuple-element.201, f32[]{:T(128)} %get-tuple-element.199, bf16[2048,768]{1,0:T(8,128)(2,1)} %get-tuple-element.200, bf16[2048,768]{1,0:T(8,128)(2,1)S(1)} %collective-permute-done), kind=kOutput, calls=%fused_computation.2.clone.1 | convolution fusion | flops 6509559808 | bytes 23068692 | tf_op jit(solution)/shard_map/while/body/eval_jaxpr/id,jd->ij/dot_general | solution.py:8
  907.2 34.7 %collective-permute-done = bf16[2048,768]{1,0:T(8,128)(2,1)S(1)} collective-permute-done((bf16[2048,768]{1,0:T(8,128)(2,1)}, bf16[2048,768]{1,0:T(8,128)(2,1)S(1)}, u32[]{:S(2)}, u32[]{:S(2)}) %collective-permute-start) | collective-permute-done | bytes 3145760 | tf_op jit(solution)/shard_map/while/body/eval_jaxpr/ppermute | solution.py:34
  1029.6 34.7 %collective-permute-done = bf16[2048,768]{1,0:T(8,128)(2,1)S(1)} collective-permute-done((bf16[2048,768]{1,0:T(8,128)(2,1)}, bf16[2048,768]{1,0:T(8,128)(2,1)S(1)}, u32[]{:S(2)}, u32[]{:S(2)}) %collective-permute-start) | collective-permute-done | bytes 3145760 | tf_op jit(solution)/shard_map/while/body/eval_jaxpr/ppermute | solution.py:34
  1064.3 24.0 %multiply_reduce_fusion.3 = (f32[]{:T(128)}, f32[]{:T(128)}, f32[]{:T(128)}, f32[2048,2048]{1,0:T(8,128)}) fusion(f32[]{:T(128)} %get-tuple-element.201, f32[]{:T(128)} %get-tuple-element.199, bf16[2048,768]{1,0:T(8,128)(2,1)} %get-tuple-element.200, bf16[2048,768]{1,0:T(8,128)(2,1)S(1)} %collective-permute-done), kind=kOutput, calls=%fused_computation.2.clone.1 | convolution fusion | flops 6509559808 | bytes 23068692 | tf_op jit(solution)/shard_map/while/body/eval_jaxpr/id,jd->ij/dot_general | solution.py:8
  1151.9 34.7 %collective-permute-done = bf16[2048,768]{1,0:T(8,128)(2,1)S(1)} collective-permute-done((bf16[2048,768]{1,0:T(8,128)(2,1)}, bf16[2048,768]{1,0:T(8,128)(2,1)S(1)}, u32[]{:S(2)}, u32[]{:S(2)}) %collective-permute-start) | collective-permute-done | bytes 3145760 | tf_op jit(solution)/shard_map/while/body/eval_jaxpr/ppermute | solution.py:34
  1274.2 34.7 %collective-permute-done = bf16[2048,768]{1,0:T(8,128)(2,1)S(1)} collective-permute-done((bf16[2048,768]{1,0:T(8,128)(2,1)}, bf16[2048,768]{1,0:T(8,128)(2,1)S(1)}, u32[]{:S(2)}, u32[]{:S(2)}) %collective-permute-start) | collective-permute-done | bytes 3145760 | tf_op jit(solution)/shard_map/while/body/eval_jaxpr/ppermute | solution.py:34
  1309.0 24.0 %multiply_reduce_fusion.3 = (f32[]{:T(128)}, f32[]{:T(128)}, f32[]{:T(128)}, f32[2048,2048]{1,0:T(8,128)}) fusion(f32[]{:T(128)} %get-tuple-element.201, f32[]{:T(128)} %get-tuple-element.199, bf16[2048,768]{1,0:T(8,128)(2,1)} %get-tuple-element.200, bf16[2048,768]{1,0:T(8,128)(2,1)S(1)} %collective-permute-done), kind=kOutput, calls=%fused_computation.2.clone.1 | convolution fusion | flops 6509559808 | bytes 23068692 | tf_op jit(solution)/shard_map/while/body/eval_jaxpr/id,jd->ij/dot_general | solution.py:8
  1396.6 34.7 %collective-permute-done = bf16[2048,768]{1,0:T(8,128)(2,1)S(1)} collective-permute-done((bf16[2048,768]{1,0:T(8,128)(2,1)}, bf16[2048,768]{1,0:T(8,128)(2,1)S(1)}, u32[]{:S(2)}, u32[]{:S(2)}) %collective-permute-start) | collective-permute-done | bytes 3145760 | tf_op jit(solution)/shard_map/while/body/eval_jaxpr/ppermute | solution.py:34
  1518.9 34.7 %collective-permute-done = bf16[2048,768]{1,0:T(8,128)(2,1)S(1)} collective-permute-done((bf16[2048,768]{1,0:T(8,128)(2,1)}, bf16[2048,768]{1,0:T(8,128)(2,1)S(1)}, u32[]{:S(2)}, u32[]{:S(2)}) %collective-permute-start) | collective-permute-done | bytes 3145760 | tf_op jit(solution)/shard_map/while/body/eval_jaxpr/ppermute | solution.py:34
  1641.2 34.7 %collective-permute-done = bf16[2048,768]{1,0:T(8,128)(2,1)S(1)} collective-permute-done((bf16[2048,768]{1,0:T(8,128)(2,1)}, bf16[2048,768]{1,0:T(8,128)(2,1)S(1)}, u32[]{:S(2)}, u32[]{:S(2)}) %collective-permute-start) | collective-permute-done | bytes 3145760 | tf_op jit(solution)/shard_map/while/body/eval_jaxpr/ppermute | solution.py:34
  1763.6 34.7 %collective-permute-done = bf16[2048,768]{1,0:T(8,128)(2,1)S(1)} collective-permute-done((bf16[2048,768]{1,0:T(8,128)(2,1)}, bf16[2048,768]{1,0:T(8,128)(2,1)S(1)}, u32[]{:S(2)}, u32[]{:S(2)}) %collective-permute-start) | collective-permute-done | bytes 3145760 | tf_op jit(solution)/shard_map/while/body/eval_jaxpr/ppermute | solution.py:34
  1887.9 93.4 %psum.7 = f32[3]{0:T(128)S(1)} all-reduce(f32[3]{0:T(128)S(1)} %pad_maximum_fusion), channel_id=1, replica_groups=mesh['dp'=16] {'dp'}, use_global_device_ids=true, to_apply=%region_8.9 | all-reduce | flops 3 | bytes 24 | tf_op jit(solution)/shard_map/psum | solution.py:42
  (142 shorter events, 1127.0 us)
Async XLA Ops:
  46.2 39.4 %collective-permute-start = (bf16[2048,768]{1,0:T(8,128)(2,1)}, bf16[2048,768]{1,0:T(8,128)(2,1)S(1)}, u32[]{:S(2)}, u32[]{:S(2)}) collective-permute-start(bf16[2048,768]{1,0:T(8,128)(2,1)} %get-tuple-element.182), channel_id=1, source_target_pairs={{0,15},{1,0},{2,1},{3,2},{4,3},{5,4},{6,5},{7,6},{8,7},{9,8},{10,9... | collective-permute-start | bytes 9437192 | tf_op jit(solution)/shard_map/while/body/eval_jaxpr/ppermute | solution.py:34
  50.9 102.2 %collective-permute-start.1 = (f32[2048,768]{1,0:T(8,128)}, f32[2048,768]{1,0:T(8,128)}, u32[]{:S(2)}, u32[]{:S(2)}) collective-permute-start(f32[2048,768]{1,0:T(8,128)} %get-tuple-element.183), channel_id=1, source_target_pairs={{0,15},{1,0},{2,1},{3,2},{4,3},{5,4},{6,5},{7,6},{8,7},{9,8},{10,9... | collective-permute-start | bytes 18874376 | tf_op jit(solution)/shard_map/while/body/eval_jaxpr/ppermute | solution.py:35
  169.5 38.5 %collective-permute-start = (bf16[2048,768]{1,0:T(8,128)(2,1)}, bf16[2048,768]{1,0:T(8,128)(2,1)S(1)}, u32[]{:S(2)}, u32[]{:S(2)}) collective-permute-start(bf16[2048,768]{1,0:T(8,128)(2,1)} %get-tuple-element.182), channel_id=1, source_target_pairs={{0,15},{1,0},{2,1},{3,2},{4,3},{5,4},{6,5},{7,6},{8,7},{9,8},{10,9... | collective-permute-start | bytes 9437192 | tf_op jit(solution)/shard_map/while/body/eval_jaxpr/ppermute | solution.py:34
  173.2 102.2 %collective-permute-start.1 = (f32[2048,768]{1,0:T(8,128)}, f32[2048,768]{1,0:T(8,128)}, u32[]{:S(2)}, u32[]{:S(2)}) collective-permute-start(f32[2048,768]{1,0:T(8,128)} %get-tuple-element.183), channel_id=1, source_target_pairs={{0,15},{1,0},{2,1},{3,2},{4,3},{5,4},{6,5},{7,6},{8,7},{9,8},{10,9... | collective-permute-start | bytes 18874376 | tf_op jit(solution)/shard_map/while/body/eval_jaxpr/ppermute | solution.py:35
  291.8 38.5 %collective-permute-start = (bf16[2048,768]{1,0:T(8,128)(2,1)}, bf16[2048,768]{1,0:T(8,128)(2,1)S(1)}, u32[]{:S(2)}, u32[]{:S(2)}) collective-permute-start(bf16[2048,768]{1,0:T(8,128)(2,1)} %get-tuple-element.182), channel_id=1, source_target_pairs={{0,15},{1,0},{2,1},{3,2},{4,3},{5,4},{6,5},{7,6},{8,7},{9,8},{10,9... | collective-permute-start | bytes 9437192 | tf_op jit(solution)/shard_map/while/body/eval_jaxpr/ppermute | solution.py:34
  295.5 102.2 %collective-permute-start.1 = (f32[2048,768]{1,0:T(8,128)}, f32[2048,768]{1,0:T(8,128)}, u32[]{:S(2)}, u32[]{:S(2)}) collective-permute-start(f32[2048,768]{1,0:T(8,128)} %get-tuple-element.183), channel_id=1, source_target_pairs={{0,15},{1,0},{2,1},{3,2},{4,3},{5,4},{6,5},{7,6},{8,7},{9,8},{10,9... | collective-permute-start | bytes 18874376 | tf_op jit(solution)/shard_map/while/body/eval_jaxpr/ppermute | solution.py:35
  414.1 38.5 %collective-permute-start = (bf16[2048,768]{1,0:T(8,128)(2,1)}, bf16[2048,768]{1,0:T(8,128)(2,1)S(1)}, u32[]{:S(2)}, u32[]{:S(2)}) collective-permute-start(bf16[2048,768]{1,0:T(8,128)(2,1)} %get-tuple-element.182), channel_id=1, source_target_pairs={{0,15},{1,0},{2,1},{3,2},{4,3},{5,4},{6,5},{7,6},{8,7},{9,8},{10,9... | collective-permute-start | bytes 9437192 | tf_op jit(solution)/shard_map/while/body/eval_jaxpr/ppermute | solution.py:34
  417.9 102.2 %collective-permute-start.1 = (f32[2048,768]{1,0:T(8,128)}, f32[2048,768]{1,0:T(8,128)}, u32[]{:S(2)}, u32[]{:S(2)}) collective-permute-start(f32[2048,768]{1,0:T(8,128)} %get-tuple-element.183), channel_id=1, source_target_pairs={{0,15},{1,0},{2,1},{3,2},{4,3},{5,4},{6,5},{7,6},{8,7},{9,8},{10,9... | collective-permute-start | bytes 18874376 | tf_op jit(solution)/shard_map/while/body/eval_jaxpr/ppermute | solution.py:35
  540.2 102.2 %collective-permute-start.1 = (f32[2048,768]{1,0:T(8,128)}, f32[2048,768]{1,0:T(8,128)}, u32[]{:S(2)}, u32[]{:S(2)}) collective-permute-start(f32[2048,768]{1,0:T(8,128)} %get-tuple-element.183), channel_id=1, source_target_pairs={{0,15},{1,0},{2,1},{3,2},{4,3},{5,4},{6,5},{7,6},{8,7},{9,8},{10,9... | collective-permute-start | bytes 18874376 | tf_op jit(solution)/shard_map/while/body/eval_jaxpr/ppermute | solution.py:35
  658.8 38.5 %collective-permute-start = (bf16[2048,768]{1,0:T(8,128)(2,1)}, bf16[2048,768]{1,0:T(8,128)(2,1)S(1)}, u32[]{:S(2)}, u32[]{:S(2)}) collective-permute-start(bf16[2048,768]{1,0:T(8,128)(2,1)} %get-tuple-element.182), channel_id=1, source_target_pairs={{0,15},{1,0},{2,1},{3,2},{4,3},{5,4},{6,5},{7,6},{8,7},{9,8},{10,9... | collective-permute-start | bytes 9437192 | tf_op jit(solution)/shard_map/while/body/eval_jaxpr/ppermute | solution.py:34
  662.5 102.2 %collective-permute-start.1 = (f32[2048,768]{1,0:T(8,128)}, f32[2048,768]{1,0:T(8,128)}, u32[]{:S(2)}, u32[]{:S(2)}) collective-permute-start(f32[2048,768]{1,0:T(8,128)} %get-tuple-element.183), channel_id=1, source_target_pairs={{0,15},{1,0},{2,1},{3,2},{4,3},{5,4},{6,5},{7,6},{8,7},{9,8},{10,9... | collective-permute-start | bytes 18874376 | tf_op jit(solution)/shard_map/while/body/eval_jaxpr/ppermute | solution.py:35
  781.1 38.5 %collective-permute-start = (bf16[2048,768]{1,0:T(8,128)(2,1)}, bf16[2048,768]{1,0:T(8,128)(2,1)S(1)}, u32[]{:S(2)}, u32[]{:S(2)}) collective-permute-start(bf16[2048,768]{1,0:T(8,128)(2,1)} %get-tuple-element.182), channel_id=1, source_target_pairs={{0,15},{1,0},{2,1},{3,2},{4,3},{5,4},{6,5},{7,6},{8,7},{9,8},{10,9... | collective-permute-start | bytes 9437192 | tf_op jit(solution)/shard_map/while/body/eval_jaxpr/ppermute | solution.py:34
  784.9 102.2 %collective-permute-start.1 = (f32[2048,768]{1,0:T(8,128)}, f32[2048,768]{1,0:T(8,128)}, u32[]{:S(2)}, u32[]{:S(2)}) collective-permute-start(f32[2048,768]{1,0:T(8,128)} %get-tuple-element.183), channel_id=1, source_target_pairs={{0,15},{1,0},{2,1},{3,2},{4,3},{5,4},{6,5},{7,6},{8,7},{9,8},{10,9... | collective-permute-start | bytes 18874376 | tf_op jit(solution)/shard_map/while/body/eval_jaxpr/ppermute | solution.py:35
  903.5 38.5 %collective-permute-start = (bf16[2048,768]{1,0:T(8,128)(2,1)}, bf16[2048,768]{1,0:T(8,128)(2,1)S(1)}, u32[]{:S(2)}, u32[]{:S(2)}) collective-permute-start(bf16[2048,768]{1,0:T(8,128)(2,1)} %get-tuple-element.182), channel_id=1, source_target_pairs={{0,15},{1,0},{2,1},{3,2},{4,3},{5,4},{6,5},{7,6},{8,7},{9,8},{10,9... | collective-permute-start | bytes 9437192 | tf_op jit(solution)/shard_map/while/body/eval_jaxpr/ppermute | solution.py:34
  907.2 102.2 %collective-permute-start.1 = (f32[2048,768]{1,0:T(8,128)}, f32[2048,768]{1,0:T(8,128)}, u32[]{:S(2)}, u32[]{:S(2)}) collective-permute-start(f32[2048,768]{1,0:T(8,128)} %get-tuple-element.183), channel_id=1, source_target_pairs={{0,15},{1,0},{2,1},{3,2},{4,3},{5,4},{6,5},{7,6},{8,7},{9,8},{10,9... | collective-permute-start | bytes 18874376 | tf_op jit(solution)/shard_map/while/body/eval_jaxpr/ppermute | solution.py:35
  1025.8 38.5 %collective-permute-start = (bf16[2048,768]{1,0:T(8,128)(2,1)}, bf16[2048,768]{1,0:T(8,128)(2,1)S(1)}, u32[]{:S(2)}, u32[]{:S(2)}) collective-permute-start(bf16[2048,768]{1,0:T(8,128)(2,1)} %get-tuple-element.182), channel_id=1, source_target_pairs={{0,15},{1,0},{2,1},{3,2},{4,3},{5,4},{6,5},{7,6},{8,7},{9,8},{10,9... | collective-permute-start | bytes 9437192 | tf_op jit(solution)/shard_map/while/body/eval_jaxpr/ppermute | solution.py:34
  1029.5 102.2 %collective-permute-start.1 = (f32[2048,768]{1,0:T(8,128)}, f32[2048,768]{1,0:T(8,128)}, u32[]{:S(2)}, u32[]{:S(2)}) collective-permute-start(f32[2048,768]{1,0:T(8,128)} %get-tuple-element.183), channel_id=1, source_target_pairs={{0,15},{1,0},{2,1},{3,2},{4,3},{5,4},{6,5},{7,6},{8,7},{9,8},{10,9... | collective-permute-start | bytes 18874376 | tf_op jit(solution)/shard_map/while/body/eval_jaxpr/ppermute | solution.py:35
  1151.9 102.2 %collective-permute-start.1 = (f32[2048,768]{1,0:T(8,128)}, f32[2048,768]{1,0:T(8,128)}, u32[]{:S(2)}, u32[]{:S(2)}) collective-permute-start(f32[2048,768]{1,0:T(8,128)} %get-tuple-element.183), channel_id=1, source_target_pairs={{0,15},{1,0},{2,1},{3,2},{4,3},{5,4},{6,5},{7,6},{8,7},{9,8},{10,9... | collective-permute-start | bytes 18874376 | tf_op jit(solution)/shard_map/while/body/eval_jaxpr/ppermute | solution.py:35
  1274.2 102.2 %collective-permute-start.1 = (f32[2048,768]{1,0:T(8,128)}, f32[2048,768]{1,0:T(8,128)}, u32[]{:S(2)}, u32[]{:S(2)}) collective-permute-start(f32[2048,768]{1,0:T(8,128)} %get-tuple-element.183), channel_id=1, source_target_pairs={{0,15},{1,0},{2,1},{3,2},{4,3},{5,4},{6,5},{7,6},{8,7},{9,8},{10,9... | collective-permute-start | bytes 18874376 | tf_op jit(solution)/shard_map/while/body/eval_jaxpr/ppermute | solution.py:35
  1396.5 102.2 %collective-permute-start.1 = (f32[2048,768]{1,0:T(8,128)}, f32[2048,768]{1,0:T(8,128)}, u32[]{:S(2)}, u32[]{:S(2)}) collective-permute-start(f32[2048,768]{1,0:T(8,128)} %get-tuple-element.183), channel_id=1, source_target_pairs={{0,15},{1,0},{2,1},{3,2},{4,3},{5,4},{6,5},{7,6},{8,7},{9,8},{10,9... | collective-permute-start | bytes 18874376 | tf_op jit(solution)/shard_map/while/body/eval_jaxpr/ppermute | solution.py:35
  1518.9 102.2 %collective-permute-start.1 = (f32[2048,768]{1,0:T(8,128)}, f32[2048,768]{1,0:T(8,128)}, u32[]{:S(2)}, u32[]{:S(2)}) collective-permute-start(f32[2048,768]{1,0:T(8,128)} %get-tuple-element.183), channel_id=1, source_target_pairs={{0,15},{1,0},{2,1},{3,2},{4,3},{5,4},{6,5},{7,6},{8,7},{9,8},{10,9... | collective-permute-start | bytes 18874376 | tf_op jit(solution)/shard_map/while/body/eval_jaxpr/ppermute | solution.py:35
  1641.2 102.2 %collective-permute-start.1 = (f32[2048,768]{1,0:T(8,128)}, f32[2048,768]{1,0:T(8,128)}, u32[]{:S(2)}, u32[]{:S(2)}) collective-permute-start(f32[2048,768]{1,0:T(8,128)} %get-tuple-element.183), channel_id=1, source_target_pairs={{0,15},{1,0},{2,1},{3,2},{4,3},{5,4},{6,5},{7,6},{8,7},{9,8},{10,9... | collective-permute-start | bytes 18874376 | tf_op jit(solution)/shard_map/while/body/eval_jaxpr/ppermute | solution.py:35
  1763.5 102.2 %collective-permute-start.1 = (f32[2048,768]{1,0:T(8,128)}, f32[2048,768]{1,0:T(8,128)}, u32[]{:S(2)}, u32[]{:S(2)}) collective-permute-start(f32[2048,768]{1,0:T(8,128)} %get-tuple-element.183), channel_id=1, source_target_pairs={{0,15},{1,0},{2,1},{3,2},{4,3},{5,4},{6,5},{7,6},{8,7},{9,8},{10,9... | collective-permute-start | bytes 18874376 | tf_op jit(solution)/shard_map/while/body/eval_jaxpr/ppermute | solution.py:35
  1882.1 107.6 %collective-permute-start.2 = (f32[2048,768]{1,0:T(8,128)}, f32[2048,768]{1,0:T(8,128)}, u32[]{:S(2)}, u32[]{:S(2)}) collective-permute-start(f32[2048,768]{1,0:T(8,128)} %get-tuple-element.65), channel_id=1, source_target_pairs={{0,15},{1,0},{2,1},{3,2},{4,3},{5,4},{6,5},{7,6},{8,7},{9,8},{10,9... | collective-permute-start | bytes 18874376 | tf_op jit(solution)/shard_map/ppermute | solution.py:41
  (24 other events, 872.8 us)
where the time goes:
time: 2000 us
  matrix products  862 us (43%)
  waiting for transfers between devices  850 us (42%)
  blocking collectives  93.4 us (5%)
  loops' own time  82.2 us (4%)
  starting transfers between devices  61.7 us (3%)
  local copies, waits for them, and re-layouts  28 us (1%)
    ppermute x15, waiting for transfers between devices, step_fn(): txt_block = lax.ppermute(txt_block, axis_name, shift_pairs)  520 us
    dot_general x16, matrix products, block_terms(): jnp.einsum('id,jd->ij', img_local, txt_block, preferred_element_type=jnp....  385 us
    ppermute x15, waiting for transfers between devices, step_fn(): txt_acc = lax.ppermute(txt_acc, axis_name, shift_pairs)  330 us
    dot_general x16, matrix products, block_terms(): jnp.einsum('ij,jd->id', coef_bf16, txt_block, preferred_element_type=jnp....  247 us
    dot_general x16, matrix products, block_terms(): jnp.einsum('ij,id->jd', coef_bf16, img_local, preferred_element_type=jnp....  230 us
    psum x1, blocking collectives, per_device(): lax.psum(jnp.stack([final_state[2], final_state[3], final_state[4]]), axi...  93.4 us
    another operation x1, loops' own time, per_device(): final_state = lax.fori_loop(1, n_dev, step_fn, init_state)  82.2 us
    ppermute x15, starting transfers between devices, step_fn(): txt_block = lax.ppermute(txt_block, axis_name, shift_pairs)  56.8 us
  transfers between devices with their start and end apart: 31, of which 30 were waited for; matrix products, arithmetic and copies ran while one was open for 32% of the time, Pallas kernels for 0%

commit v1 on v0

v1 whole, which is shorter than its diff:
```python
import jax
import jax.numpy as jnp
from jax import lax
from jax.experimental import pallas as pl
from jax.experimental.pallas import tpu as pltpu
from jax.sharding import PartitionSpec as P

LOG2E = 1.4426950408889634
LN2 = 0.6931471805599453
BQ = 1024
BK = 512
CLAMP = 30.0
NT = (((1,), (1,)), ((), ()))
NN = (((1,), (0,)), ((), ()))


def fold(z):
    rows, cols = z.shape
    if cols > 128:
        z = sum(z[:, c:c + 128] for c in range(0, cols, 128))
    return jnp.sum(z.reshape(rows // 8, 8, 128), axis=0)


def log_one_plus(x):
    w = 1.0 + x
    return jnp.log(w) + jnp.where(x < 1.0, x - (w - 1.0), 0.0)


def pair_terms(tx, ty):
    ex, ey = jnp.exp2(tx), jnp.exp2(ty)
    ay = 1.0 + ey
    w = ex * ay
    q = w + ey
    d = 1.0 + q
    r = 1.0 / d
    return w * r, (ey * (1.0 + ex)) * r, q, d


def logits(s_ref, k, a, b2, offset):
    quarter = BK // 4
    dot = s_ref[:, k * quarter:(k + 1) * quarter]
    t = a * dot + b2
    if offset is None:
        return dot, t, None
    rows = lax.broadcasted_iota(jnp.int32, dot.shape, 0)
    cols = lax.broadcasted_iota(jnp.int32, dot.shape, 1) + k * quarter
    match = rows - cols == offset
    return dot, jnp.where(match, -t, t), match


def img_elem(s_ref, c_ref, sums_ref, a, b2, offset):
    quarter = BK // 4
    dots, ts, matches = zip(*[logits(s_ref, k, a, b2, offset) for k in range(4)])
    tc = [jnp.minimum(t, CLAMP) for t in ts]
    p0, p1, q01, _ = pair_terms(tc[0], tc[1])
    p2, p3, q23, d23 = pair_terms(tc[2], tc[3])
    ps = [p0, p1, p2, p3]
    if offset is not None:
        ps = [jnp.where(m, -p, p) for m, p in zip(matches, ps)]
    q4 = q01 * d23 + q23
    over = [t - c for t, c in zip(ts, tc)]
    sums_ref[0] += fold(log_one_plus(q4) + LN2 * ((over[0] + over[1]) + (over[2] + over[3])))
    sums_ref[1] += fold((ps[0] + ps[1]) + (ps[2] + ps[3]))
    sums_ref[2] += fold((ps[0] * dots[0] + ps[1] * dots[1]) + (ps[2] * dots[2] + ps[3] * dots[3]))
    for k in range(4):
        c_ref[:, k * quarter:(k + 1) * quarter] = ps[k].astype(jnp.bfloat16)


def txt_elem(s_ref, c_ref, a, b2, offset):
    quarter = BK // 4
    for k in range(0, 4, 2):
        _, tx, mx = logits(s_ref, k, a, b2, offset)
        _, ty, my = logits(s_ref, k + 1, a, b2, offset)
        px, py, _, _ = pair_terms(jnp.minimum(tx, 2 * CLAMP), jnp.minimum(ty, 2 * CLAMP))
        if offset is not None:
            px, py = jnp.where(mx, -px, px), jnp.where(my, -py, py)
        c_ref[:, k * quarter:(k + 1) * quarter] = px.astype(jnp.bfloat16)
        c_ref[:, (k + 1) * quarter:(k + 2) * quarter] = py.astype(jnp.bfloat16)


def kernel(coef, q0_ref, q1_ref, k0_ref, k1_ref, out0_ref, out1_ref, sums_ref, kb0, kb1, s00, s01, s10, s11, c00, c01, c10, c11, ksem):
    nkb = k0_ref.shape[0] // BK
    rows_local = q0_ref.shape[0]
    nq = rows_local // BQ
    own_steps = (rows_local // BK) * nq
    total = nkb * nq
    a, b2 = coef[0], coef[1]
    me = lax.axis_index('dp')

    def fetch(j):
        sl = lax.rem(j, 3)
        row = pl.multiple_of(lax.rem(me * rows_local + j * BK, k0_ref.shape[0]), BK)
        return [pltpu.make_async_copy(k.at[pl.ds(row, BK), :], kb.at[sl], ksem.at[i, sl]) for i, (k, kb) in enumerate(((k0_ref, kb0), (k1_ref, kb1)))]

    sums_ref[...] = jnp.zeros_like(sums_ref)
    out0_ref[...] = jnp.zeros_like(out0_ref)
    out1_ref[...] = jnp.zeros_like(out1_ref)
    c01[...] = jnp.zeros_like(c01)
    c11[...] = jnp.zeros_like(c11)
    for c in fetch(0) + fetch(1):
        c.start()
    for c in fetch(0):
        c.wait()
    s00[...] = lax.dot_general(q0_ref[0:BQ, :], kb0[0], NT, preferred_element_type=jnp.float32)
    s10[...] = lax.dot_general(q1_ref[0:BQ, :], kb1[0], NT, preferred_element_type=jnp.float32)

    def grads(qp, sp, o, ci, kb):
        o[pl.ds(qp, BQ), :] += lax.dot_general(ci[...], kb[sp], NN, preferred_element_type=jnp.float32)

    def step(t, s0i, s0o, s1i, s1o, c0i, c0o, c1i, c1o, own):
        t_next = jnp.minimum(t + 1, total - 1)
        t_prev = jnp.maximum(t - 1, 0)
        qn = pl.multiple_of(lax.rem(t_next, nq) * BQ, BQ)
        qp = pl.multiple_of(lax.rem(t_prev, nq) * BQ, BQ)
        sn = lax.rem(lax.div(t_next, nq), 3)
        sp = lax.rem(lax.div(t_prev, nq), 3)
        offset = lax.div(t, nq) * BK - lax.rem(t, nq) * BQ if own else None
        s0o[...] = lax.dot_general(q0_ref[pl.ds(qn, BQ), :], kb0[sn], NT, preferred_element_type=jnp.float32)
        img_elem(s0i, c0o, sums_ref, a, b2, offset)
        grads(qp, sp, out0_ref, c0i, kb0)
        s1o[...] = lax.dot_general(q1_ref[pl.ds(qn, BQ), :], kb1[sn], NT, preferred_element_type=jnp.float32)
        txt_elem(s1i, c1o, a, b2, offset)
        grads(qp, sp, out1_ref, c1i, kb1)

    def body(own):
        def run(h, _):
            j = h

            @pl.when(j + 1 < nkb)
            def _():
                for c in fetch(j + 1):
                    c.wait()

            step(2 * h, s00, s01, s10, s11, c01, c00, c11, c10, own)

            @pl.when(j + 2 < nkb)
            def _():
                for c in fetch(j + 2):
                    c.start()

            step(2 * h + 1, s01, s00, s11, s10, c00, c01, c10, c11, own)
            return 0
        return run

    lax.fori_loop(0, own_steps // 2, body(True), 0)
    lax.fori_loop(own_steps // 2, total // 2, body(False), 0)
    grads((nq - 1) * BQ, (nkb - 1) % 3, out0_ref, c01, kb0)
    grads((nq - 1) * BQ, (nkb - 1) % 3, out1_ref, c11, kb1)


def both_sides(coef, q0, q1, k0, k1):
    rows, depth = q0.shape
    in_vmem = pl.BlockSpec(memory_space=pltpu.VMEM)
    anywhere = pl.BlockSpec(memory_space=pl.ANY)
    grad = jax.ShapeDtypeStruct((rows, depth), jnp.float32)
    return pl.pallas_call(
        kernel,
        out_shape=(grad, grad, jax.ShapeDtypeStruct((3, 8, 128), jnp.float32)),
        in_specs=[pl.BlockSpec(memory_space=pltpu.SMEM), in_vmem, in_vmem, anywhere, anywhere],
        out_specs=(in_vmem, in_vmem, in_vmem),
        scratch_shapes=[pltpu.VMEM((3, BK, depth), jnp.bfloat16)] * 2
        + [pltpu.VMEM((BQ, BK), jnp.float32)] * 4
        + [pltpu.VMEM((BQ, BK), jnp.bfloat16)] * 4
        + [pltpu.SemaphoreType.DMA((2, 3))],
        compiler_params=pltpu.CompilerParams(vmem_limit_bytes=62 * 1024 * 1024),
    )(coef, q0, q1, k0, k1)


def solution(mesh):
    axis_name = mesh.axis_names[0]
    n_dev = mesh.shape[axis_name]

    def per_device(img, txt, log_temp, logit_bias):
        n_total = img.shape[0] * n_dev
        scale = jnp.exp(log_temp[0])
        coef = jnp.stack([scale * LOG2E, logit_bias[0] * LOG2E])
        txt_all = lax.all_gather(txt, axis_name, tiled=True)
        img_all = lax.all_gather(img, axis_name, tiled=True)
        img_sum, txt_sum, sums = both_sides(coef, img, txt, txt_all, img_all)
        factor = scale / n_total
        totals = lax.psum(jnp.sum(sums, axis=(1, 2)), axis_name)
        return totals[0:1] / n_total, img_sum * factor, txt_sum * factor, totals[2:3] * factor, totals[1:2] / n_total

    return jax.shard_map(per_device, mesh=mesh, in_specs=(P(axis_name, None), P(axis_name, None), P(None), P(None)), out_specs=(P(None), P(axis_name, None), P(axis_name, None), P(None), P(None)), check_vma=False)
```

time: 2000 us -> 944 us (0.47)
  matrix products: 862 us -> 0 us
  Pallas kernels: 0 us -> 500 us
  waiting for transfers between devices: 850 us -> 378 us
  loops' own time: 82.2 us -> 0 us
  starting transfers between devices: 61.7 us -> 0.08 us
  blocking collectives: 93.4 us -> 31.8 us
  local copies, waits for them, and re-layouts: 28 us -> 0.59 us
    dot_general x48 -> x0, matrix products: 862 us -> none  [the longest x16 385 us: block_terms(): jnp.einsum('id,jd->ij', img_local, txt_block, preferred_element_type=jnp....]
    ppermute x31 -> x0, waiting for transfers between devices: 850 us -> none  [the longest x15 520 us: step_fn(): txt_block = lax.ppermute(txt_block, axis_name, shift_pairs)]
    pallas_call x0 -> x1, Pallas kernels: none -> 500 us  [both_sides(): pl.pallas_call(kernel, out_shape=(grad, grad, jax.ShapeDtypeStruct((3, 8,...]
    all_gather x0 -> x2, waiting for transfers between devices: none -> 377 us  [the longest x1 189 us: per_device(): img_all = lax.all_gather(img, axis_name, tiled=True)]
    another operation x1 -> x0, loops' own time: 82.2 us -> none  [per_device(): final_state = lax.fori_loop(1, n_dev, step_fn, init_state)]
    ppermute x31 -> x0, starting transfers between devices: 61.7 us -> none  [the longest x15 56.8 us: step_fn(): txt_block = lax.ppermute(txt_block, axis_name, shift_pairs)]
    psum x1, blocking collectives: 93.4 us -> 31.8 us  [per_device(): totals = lax.psum(jnp.sum(sums, axis=(1, 2)), axis_name)]
    while x45 -> x0, local copies, waits for them, and re-layouts: 25.6 us -> none
  transfers between devices with their start and end apart: 31 -> 2, of which waited for: 30 -> 2; matrix products, arithmetic and copies ran while one was open for 32% -> 0% of each run, Pallas kernels for 0% -> 0%
where the time goes in v1:
time: 944 us
  Pallas kernels  500 us (53%)
  waiting for transfers between devices  378 us (40%)
  blocking collectives  31.8 us (3%)
  between operations  20.7 us (2%)
  other arithmetic  11.6 us (1%)
    pallas_call x1, Pallas kernels, both_sides(): pl.pallas_call(kernel, out_shape=(grad, grad, jax.ShapeDtypeStruct((3, 8,...  500 us
    all_gather x1, waiting for transfers between devices, per_device(): img_all = lax.all_gather(img, axis_name, tiled=True)  189 us
    all_gather x1, waiting for transfers between devices, per_device(): txt_all = lax.all_gather(txt, axis_name, tiled=True)  188 us
    psum x1, blocking collectives, per_device(): totals = lax.psum(jnp.sum(sums, axis=(1, 2)), axis_name)  31.8 us
  transfers between devices with their start and end apart: 2, of which 2 were waited for; matrix products, arithmetic and copies ran while one was open for 0% of the time, Pallas kernels for 0%

profile of v1, /device:TPU:0, one launch (start us, length us, event | category | flops | bytes accessed | tf_op | source)
XLA Modules:
  0.0 943.6 jit_solution(2672456302247872132)
XLA Ops:
  7.2 0.0 all-gather.5.cloned.1.call-start
  7.2 0.7 all-gather.5.cloned.1.call-update
  7.9 0.0 all-gather.3.cloned.1.call-start
  7.9 0.7 all-gather.3.cloned.1.call-update
  10.0 0.6 pad_maximum_fusion.coef
  10.6 188.6 %all-gather.5.cloned.1.call-done.k1_ref = bf16[32768,768]{1,0:T(8,128)(2,1)} async-done(((bf16[2048,768]{1,0:T(8,128)(2,1)}), bf16[32768,768]{1,0:T(8,128)(2,1)}) %all-gather.5.cloned.1.call-update) | async-done | bytes 50331664 | tf_op jit(solution)/shard_map/all_gather | solution.py:178
  199.2 188.4 %all-gather.3.cloned.1.call-done.k0_ref = bf16[32768,768]{1,0:T(8,128)(2,1)} async-done(((bf16[2048,768]{1,0:T(8,128)(2,1)}), bf16[32768,768]{1,0:T(8,128)(2,1)}) %all-gather.3.cloned.1.call-update) | async-done | bytes 50331664 | tf_op jit(solution)/shard_map/all_gather | solution.py:177
  387.6 500.5 %shard_map.83 = (f32[2048,768]{1,0:T(8,128)}, f32[2048,768]{1,0:T(8,128)}, f32[3,8,128]{2,1,0:T(8,128)}) custom-call(f32[2]{0:T(128)} %pad_maximum_fusion.coef, bf16[2048,768]{1,0:T(8,128)(2,1)} %q0_ref.1, bf16[2048,768]{1,0:T(8,128)(2,1)} %q1_ref.1, bf16[32768,768]{1,0:T(8,128)(2,1)} %all-gather.3.cloned.1.call-done.k0_ref, ...), custom_call_target="tpu_custom_call" | custom-call | tf_op jit(solution)/shard_map/pallas_call | solution.py:156
  888.1 0.8 reduce_sum.9
  888.9 31.8 %psum.7 = f32[3]{0:T(128)S(1)} all-reduce(f32[3]{0:T(128)S(1)} %reduce_sum.9), channel_id=1, replica_groups=mesh['dp'=16] {'dp'}, use_global_device_ids=true, to_apply=%region_1.0 | all-reduce | flops 3 | bytes 24 | tf_op jit(solution)/shard_map/psum | solution.py:181
  920.7 0.6 fusion
  923.2 10.2 %broadcast_multiply_fusion = (f32[2048,768]{1,0:T(8,128)}, f32[2048,768]{1,0:T(8,128)}) fusion(f32[2048,768]{1,0:T(8,128)} %get-tuple-element.10, f32[]{:T(128)} %bitcast, f32[2048,768]{1,0:T(8,128)} %get-tuple-element.9), kind=kLoop, calls=%fused_computation | loop fusion | flops 3145728 | bytes 25165828 | tf_op jit(solution)/shard_map/mul | solution.py:182
Async XLA Ops:
  7.2 192.0 %all-gather.5.cloned.1.call-start = ((), (), s32[]{:S(2)}) async-start(), calls=%async_computation.1 | async-start | bytes 53477376 | tf_op jit(solution)/shard_map/all_gather | solution.py:178
  7.9 379.7 %all-gather.3.cloned.1.call-start = ((), (), s32[]{:S(2)}) async-start(), calls=%async_computation | async-start | bytes 53477376 | tf_op jit(solution)/shard_map/all_gather | solution.py:177
Sparse Core Ops, SparseCore 0:
  10.2 188.9 all-gather.4
  201.4 186.1 all-gather.2

commit v2 on v1

v2 whole, which is shorter than its diff:
```python
import jax
import jax.numpy as jnp
from jax import lax
from jax.experimental import pallas as pl
from jax.experimental.pallas import tpu as pltpu
from jax.sharding import PartitionSpec as P

LOG2E = 1.4426950408889634
LN2 = 0.6931471805599453
BQ = 1024
BK = 512
CLAMP = 30.0
NT = (((1,), (1,)), ((), ()))
NN = (((1,), (0,)), ((), ()))


def fold(z):
    rows, cols = z.shape
    if cols > 128:
        z = sum(z[:, c:c + 128] for c in range(0, cols, 128))
    return jnp.sum(z.reshape(rows // 8, 8, 128), axis=0)


def log_one_plus(x):
    w = 1.0 + x
    return jnp.log(w) + jnp.where(x < 1.0, x - (w - 1.0), 0.0)


def joint(ex, ey):
    return ex * (1.0 + ey) + ey


def logits(s_ref, k, a, b2, offset):
    quarter = BK // 4
    dot = s_ref[:, k * quarter:(k + 1) * quarter]
    t = a * dot + b2
    if offset is None:
        return dot, t, None
    rows = lax.broadcasted_iota(jnp.int32, dot.shape, 0)
    cols = lax.broadcasted_iota(jnp.int32, dot.shape, 1) + k * quarter
    match = rows - cols == offset
    return dot, jnp.where(match, -t, t), match


def img_elem(s_ref, c_ref, sums_ref, a, b2, offset):
    quarter = BK // 4
    dots, ts, matches = zip(*[logits(s_ref, k, a, b2, offset) for k in range(4)])
    tc = [jnp.minimum(t, CLAMP) for t in ts]
    es = [jnp.exp2(t) for t in tc]
    ps = [e * (1.0 / (1.0 + e)) for e in es]
    if offset is not None:
        ps = [jnp.where(m, -p, p) for m, p in zip(matches, ps)]
    q4 = joint(joint(es[0], es[1]), joint(es[2], es[3]))
    over = [t - c for t, c in zip(ts, tc)]
    sums_ref[0] += fold(log_one_plus(q4) + LN2 * ((over[0] + over[1]) + (over[2] + over[3])))
    sums_ref[1] += fold((ps[0] + ps[1]) + (ps[2] + ps[3]))
    sums_ref[2] += fold((ps[0] * dots[0] + ps[1] * dots[1]) + (ps[2] * dots[2] + ps[3] * dots[3]))
    for k in range(4):
        c_ref[:, k * quarter:(k + 1) * quarter] = ps[k].astype(jnp.bfloat16)


def txt_elem(s_ref, c_ref, a, b2, offset):
    quarter = BK // 4
    for k in range(4):
        _, t, match = logits(s_ref, k, -a, -b2, offset)
        p = 1.0 / (1.0 + jnp.exp2(t))
        if offset is not None:
            p = jnp.where(match, -p, p)
        c_ref[:, k * quarter:(k + 1) * quarter] = p.astype(jnp.bfloat16)


def kernel(coef, q0_ref, q1_ref, own0_ref, own1_ref, out0_ref, out1_ref, sums_ref, all0_ref, all1_ref, kb0, kb1, s00, s01, s10, s11, c00, c01, c10, c11, ksem, hop_send, hop_recv, pair_send, pair_recv, part_ref, gathered, sum_send, sum_recv, free):
    rows_local = q0_ref.shape[0]
    nq = rows_local // BQ
    parts = rows_local // BK
    chips = all0_ref.shape[0] // rows_local
    n_dev = 2 * chips
    nkb = n_dev * parts
    total = nkb * nq
    a, b2 = coef[0], coef[1]
    me = lax.axis_index('dp')
    core, chip = lax.rem(me, 2), lax.div(me, 2)
    partner = me + 1 - 2 * core
    owns, alls, kbs, locals_ = (own0_ref, own1_ref), (all0_ref, all1_ref), (kb0, kb1), (q1_ref, q0_ref)

    def remote(source, target, send, recv, device):
        return pltpu.make_async_remote_copy(source, target, send, recv, device_id=(device,), device_id_type=pl.DeviceIdType.MESH)

    def weights(part, side):
        result = []
        for k in range(3):
            axis = jnp.where(part == 3, 2 - k if side == 0 else k, lax.rem(part + k, 3))
            weight = 1 + axis + lax.div(axis, 2)
            result.append(weight * (1 - 2 * lax.rem(lax.div(chip, weight), 2)))
        return result

    def place(route, part, side):
        bits = (lax.rem(route, 2), lax.rem(lax.div(route, 2), 2), lax.div(route, 4))
        source = chip
        for bit, flip in zip(bits, weights(part, side)):
            source = source + bit * flip
        return pl.ds(pl.multiple_of(source * rows_local + part * BK, BK), BK)

    def message(route, part, side):
        return (route * parts + part) * 2 + side

    def local_rows(part, side):
        return locals_[side].at[pl.ds(pl.multiple_of(part * BK, BK), BK), :]

    def hop(route, k, part, side, own=False):
        index = message(route + (1 << k), part, side)
        rows = alls[side].at[place(route, part, side), :]
        return remote(local_rows(part, side) if own else rows, rows, hop_send.at[index], hop_recv.at[index], me + 2 * weights(part, side)[k])

    def hop_arrival(route, part, side):
        index = message(route, part, side)
        rows = alls[side].at[place(route, part, side), :]
        return remote(rows, rows, hop_send.at[index], hop_recv.at[index], partner)

    def pair(route, part, side, source):
        index = message(route, part, side)
        return remote(source, kbs[side].at[3 + part], pair_send.at[index], pair_recv.at[index], partner)

    def stage_of(j):
        return lax.div(j, 2 * parts)

    def route_of(j):
        i = stage_of(j)
        return i + jnp.where(i == 3, 1, 0) - jnp.where(i == 4, 1, 0)

    def part_of(j):
        return lax.rem(j, parts)

    def from_partner(j):
        return lax.rem(lax.div(j, parts), 2) == 1

    def ring(j):
        return lax.rem(stage_of(j) * parts + part_of(j), 3)

    def slot(j):
        return jnp.where(from_partner(j), 3 + part_of(j), ring(j))

    def fetch_own(j):
        row = pl.multiple_of(part_of(j) * BK, BK)
        return [pltpu.make_async_copy(owns[side].at[pl.ds(row, BK), :], kbs[side].at[ring(j)], ksem.at[side, ring(j)]) for side in range(2)]

    def fetch(j):
        return [pltpu.make_async_copy(alls[side].at[place(route_of(j), part_of(j), side), :], kbs[side].at[ring(j)], ksem.at[side, ring(j)]) for side in range(2)]

    def pair_block(j, side):
        return pair(route_of(j), part_of(j), side, kbs[side].at[ring(j)])

    def make_ready(j):
        partner_block = from_partner(j)

        @pl.when(partner_block)
        def _():
            for side in range(2):
                pair_block(j, side).wait_recv()

        @pl.when(jnp.logical_not(partner_block))
        def _():
            for c in fetch(j):
                c.wait()
            pl.semaphore_wait(free.at[part_of(j)], 1)
            for side in range(2):
                pair_block(j, side).start()

    def prefetch(j):
        route, part = route_of(j), part_of(j)
        for side in range(2):
            hop_arrival(route, part, side).wait_recv()
        for k in range(1, 3):
            @pl.when(route < (1 << k))
            def _():
                for side in range(2):
                    hop(route, k, part, side).start()

        @pl.when(stage_of(j) * parts + part - 3 >= parts)
        def _():
            back = jnp.where(part == 3, j - 3, j - 2 * parts + 1)
            for side in range(2):
                pair_block(back, side).wait_send()
        for c in fetch(j):
            c.start()

    barrier = pltpu.get_barrier_semaphore()

    def greet(n, _):
        pl.semaphore_signal(barrier, inc=1, device_id=(lax.rem(me + n, n_dev),), device_id_type=pl.DeviceIdType.MESH)
        return 0

    lax.fori_loop(1, n_dev, greet, 0)
    for c in fetch_own(0) + fetch_own(1):
        c.start()
    pl.semaphore_wait(barrier, n_dev - 1)

    def start_own(part, _):
        for side in range(2):
            hop(0, 0, part, side, own=True).start()
        for side in range(2):
            pair(0, part, side, local_rows(part, side)).start()
        return 0

    def start_later(part, _):
        for k in range(1, 3):
            for side in range(2):
                hop(0, k, part, side, own=True).start()
        return 0

    lax.fori_loop(0, parts, start_own, 0)
    lax.fori_loop(0, parts, start_later, 0)

    part_ref[...] = jnp.zeros_like(part_ref)
    out0_ref[...] = jnp.zeros_like(out0_ref)
    out1_ref[...] = jnp.zeros_like(out1_ref)
    c01[...] = jnp.zeros_like(c01)
    c11[...] = jnp.zeros_like(c11)
    for c in fetch_own(0):
        c.wait()
    s00[...] = lax.dot_general(q0_ref[0:BQ, :], kb0[0], NT, preferred_element_type=jnp.float32)
    s10[...] = lax.dot_general(q1_ref[0:BQ, :], kb1[0], NT, preferred_element_type=jnp.float32)

    def grads(qp, sp, o, ci, kb):
        o[pl.ds(qp, BQ), :] += lax.dot_general(ci[...], kb[sp], NN, preferred_element_type=jnp.float32)

    def step(t, s0i, s0o, s1i, s1o, c0i, c0o, c1i, c1o, own):
        t_next = jnp.minimum(t + 1, total - 1)
        t_prev = jnp.maximum(t - 1, 0)
        qn = pl.multiple_of(lax.rem(t_next, nq) * BQ, BQ)
        qp = pl.multiple_of(lax.rem(t_prev, nq) * BQ, BQ)
        sn = slot(lax.div(t_next, nq))
        sp = slot(lax.div(t_prev, nq))
        offset = lax.div(t, nq) * BK - lax.rem(t, nq) * BQ if own else None
        s0o[...] = lax.dot_general(q0_ref[pl.ds(qn, BQ), :], kb0[sn], NT, preferred_element_type=jnp.float32)
        img_elem(s0i, c0o, part_ref, a, b2, offset)
        grads(qp, sp, out0_ref, c0i, kb0)
        s1o[...] = lax.dot_general(q1_ref[pl.ds(qn, BQ), :], kb1[sn], NT, preferred_element_type=jnp.float32)
        txt_elem(s1i, c1o, a, b2, offset)
        grads(qp, sp, out1_ref, c1i, kb1)

    def own_body(j, _):
        @pl.when(j + 1 < parts)
        def _():
            for c in fetch_own(j + 1):
                c.wait()

        @pl.when(j + 1 == parts)
        def _():
            for side in range(2):
                pair(0, 0, side, local_rows(0, side)).wait_recv()

        step(2 * j, s00, s01, s10, s11, c01, c00, c11, c10, True)

        @pl.when(j + 2 < parts)
        def _():
            for c in fetch_own(j + 2):
                c.start()

        step(2 * j + 1, s01, s00, s11, s10, c00, c01, c10, c11, True)
        return 0

    def body(j, _):
        @pl.when(j + 1 < nkb)
        def _():
            make_ready(j + 1)

        step(2 * j, s00, s01, s10, s11, c01, c00, c11, c10, False)

        @pl.when(jnp.logical_and(from_partner(j - 1), j - 1 < nkb - parts))
        def _():
            pl.semaphore_signal(free.at[part_of(j - 1)], inc=1, device_id=(partner,), device_id_type=pl.DeviceIdType.MESH)

        @pl.when(jnp.logical_and(j + 2 < nkb, jnp.logical_not(from_partner(j + 2))))
        def _():
            prefetch(j + 2)

        step(2 * j + 1, s01, s00, s11, s10, c00, c01, c10, c11, False)
        return 0

    lax.fori_loop(0, parts, own_body, 0)
    lax.fori_loop(parts, nkb, body, 0)
    last = slot(nkb - 1)
    grads((nq - 1) * BQ, last, out0_ref, c01, kb0)

    def share(target, sender):
        return remote(part_ref, gathered.at[sender], sum_send.at[target], sum_recv.at[sender], target)

    def share_start(n, _):
        share(lax.rem(me + n, n_dev), me).start()
        return 0

    def share_wait(n, _):
        other = lax.rem(me + n, n_dev)
        share(other, other).wait_recv()
        share(other, me).wait_send()
        return 0

    lax.fori_loop(1, n_dev, share_start, 0)
    gathered[me] = part_ref[...]
    grads((nq - 1) * BQ, last, out1_ref, c11, kb1)
    lax.fori_loop(1, n_dev, share_wait, 0)
    sums_ref[...] = jnp.sum(gathered[...], axis=0)

    def drain_hops(n, _):
        for side in range(2):
            hop_arrival(lax.div(n, parts), lax.rem(n, parts), side).wait_send()
        return 0

    def drain_first(part, _):
        for side in range(2):
            pair(0, part, side, local_rows(part, side)).wait_send()
        return 0

    def drain_last(part, _):
        for side in range(2):
            pair_block(nkb - 2 * parts + part, side).wait_send()
        return 0

    lax.fori_loop(parts, chips * parts, drain_hops, 0)
    lax.fori_loop(0, parts, drain_first, 0)
    lax.fori_loop(1, parts, drain_last, 0)


def both_sides(coef, img, txt, n_dev):
    rows, depth = img.shape
    in_vmem = pl.BlockSpec(memory_space=pltpu.VMEM)
    anywhere = pl.BlockSpec(memory_space=pl.ANY)
    grad = jax.ShapeDtypeStruct((rows, depth), jnp.float32)
    whole = jax.ShapeDtypeStruct((rows * (n_dev // 2), depth), img.dtype)
    messages = 8 * (rows // BK) * 2
    return pl.pallas_call(
        kernel,
        out_shape=(grad, grad, jax.ShapeDtypeStruct((3, 8, 128), jnp.float32), whole, whole),
        in_specs=[pl.BlockSpec(memory_space=pltpu.SMEM), in_vmem, in_vmem, anywhere, anywhere],
        out_specs=(in_vmem, in_vmem, in_vmem, anywhere, anywhere),
        scratch_shapes=[pltpu.VMEM((3 + rows // BK, BK, depth), jnp.bfloat16)] * 2
        + [pltpu.VMEM((BQ, BK), jnp.float32)] * 4
        + [pltpu.VMEM((BQ, BK), jnp.bfloat16)] * 4
        + [pltpu.SemaphoreType.DMA((2, 3))]
        + [pltpu.SemaphoreType.DMA((messages,))] * 4
        + [pltpu.VMEM((3, 8, 128), jnp.float32), pltpu.VMEM((n_dev, 3, 8, 128), jnp.float32)]
        + [pltpu.SemaphoreType.DMA((n_dev,))] * 2
        + [pltpu.SemaphoreType.REGULAR((rows // BK,))],
        compiler_params=pltpu.CompilerParams(vmem_limit_bytes=62 * 1024 * 1024, collective_id=0, has_side_effects=True),
    )(coef, img, txt, txt, img)


def solution(mesh):
    axis_name = mesh.axis_names[0]
    n_dev = mesh.shape[axis_name]

    def per_device(img, txt, log_temp, logit_bias):
        n_total = img.shape[0] * n_dev
        scale = jnp.exp(log_temp[0])
        coef = jnp.stack([scale * LOG2E, logit_bias[0] * LOG2E])
        img_sum, txt_sum, sums, _, _ = both_sides(coef, img, txt, n_dev)
        factor = scale / n_total
        totals = jnp.sum(sums, axis=(1, 2))
        return totals[0:1] / n_total, img_sum * factor, txt_sum * factor, totals[2:3] * factor, totals[1:2] / n_total

    return jax.shard_map(per_device, mesh=mesh, in_specs=(P(axis_name, None), P(axis_name, None), P(None), P(None)), out_specs=(P(None), P(axis_name, None), P(axis_name, None), P(None), P(None)), check_vma=False)
```

time: 944 us -> 732 us (0.78)
  waiting for transfers between devices: 378 us -> 0 us
  Pallas kernels: 500 us -> 712 us
  blocking collectives: 31.8 us -> 0 us
  between operations: 20.7 us -> 7.31 us
    all_gather x2 -> x0, waiting for transfers between devices: 377 us -> none  [the longest x1 189 us: per_device(): img_all = lax.all_gather(img, axis_name, tiled=True)]
    pallas_call x1, Pallas kernels: 500 us -> 712 us  [both_sides(): pl.pallas_call(kernel, out_shape=(grad, grad, jax.ShapeDtypeStruct((3, 8,...]
    psum x1 -> x0, blocking collectives: 31.8 us -> none  [per_device(): totals = lax.psum(jnp.sum(sums, axis=(1, 2)), axis_name)]
  transfers between devices with their start and end apart: 2 -> 0, of which waited for: 2 -> 0; matrix products, arithmetic and copies ran while one was open for 0% -> 0% of each run, Pallas kernels for 0% -> 0%
where the time goes in v2:
time: 732 us; the launch traced here: 731 us
  Pallas kernels  712 us (97%)
  other arithmetic  11.6 us (2%)
    pallas_call x1, Pallas kernels, both_sides(): pl.pallas_call(kernel, out_shape=(grad, grad, jax.ShapeDtypeStruct((3, 8,...  712 us

profile of v2, /device:TPU:0, one launch (start us, length us, event | category | flops | bytes accessed | tf_op | source)
XLA Modules:
  0.0 731.3 jit_solution(13130542187681709962)
XLA Ops:
  2.0 0.6 pad_maximum_fusion.coef
  2.6 711.8 %shard_map.83 = (f32[2048,768]{1,0:T(8,128)}, f32[2048,768]{1,0:T(8,128)}, f32[3,8,128]{2,1,0:T(8,128)}, bf16[16384,768]{1,0:T(8,128)(2,1)}, bf16[16384,768]{1,0:T(8,128)(2,1)}) custom-call(f32[2]{0:T(128)} %pad_maximum_fusion.coef, bf16[2048,768]{1,0:T(8,128)(2,1)} %own1_ref.1, bf16[2048,768]{1,0:T(8,128)(2,1)} %own0_ref.1, bf16[2048,768]{1,0:T(8,128)(2,1)} %own0_ref.1, ...), custom_call_target="tpu_custom_call" | custom-call | tf_op jit(solution)/shard_map/pallas_call | solution.py:332
  714.4 0.8 reduce_sum.9
  715.2 0.6 fusion
  717.7 10.2 %broadcast_multiply_fusion = (f32[2048,768]{1,0:T(8,128)}, f32[2048,768]{1,0:T(8,128)}) fusion(f32[2048,768]{1,0:T(8,128)} %get-tuple-element.10, f32[]{:T(128)} %bitcast, f32[2048,768]{1,0:T(8,128)} %get-tuple-element.9), kind=kLoop, calls=%fused_computation | loop fusion | flops 3145728 | bytes 25165828 | tf_op jit(solution)/shard_map/mul | solution.py:360

commit v3 on v2

--- a/solution.py
+++ b/solution.py
@@ -119,7 +119,7 @@
 
     def pair(route, part, side, source):
         index = message(route, part, side)
-        return remote(source, kbs[side].at[3 + part], pair_send.at[index], pair_recv.at[index], partner)
+        return remote(source, kbs[side].at[parts + part], pair_send.at[index], pair_recv.at[index], partner)
 
     def stage_of(j):
         return lax.div(j, 2 * parts)
@@ -135,10 +135,10 @@
         return lax.rem(lax.div(j, parts), 2) == 1
 
     def ring(j):
-        return lax.rem(stage_of(j) * parts + part_of(j), 3)
+        return part_of(j)
 
     def slot(j):
-        return jnp.where(from_partner(j), 3 + part_of(j), ring(j))
+        return lax.rem(j, 2 * parts)
 
     def fetch_own(j):
         row = pl.multiple_of(part_of(j) * BK, BK)
@@ -176,11 +176,10 @@
                 for side in range(2):
                     hop(route, k, part, side).start()
 
-        @pl.when(stage_of(j) * parts + part - 3 >= parts)
-        def _():
-            back = jnp.where(part == 3, j - 3, j - 2 * parts + 1)
-            for side in range(2):
-                pair_block(back, side).wait_send()
+        @pl.when(stage_of(j) >= 2)
+        def _():
+            for side in range(2):
+                pair_block(j - 2 * parts, side).wait_send()
         for c in fetch(j):
             c.start()
 
@@ -265,16 +264,15 @@
         def _():
             make_ready(j + 1)
 
+        @pl.when(jnp.logical_and(from_partner(j - 2), j - 2 < nkb - parts))
+        def _():
+            pl.semaphore_signal(free.at[part_of(j - 2)], inc=1, device_id=(partner,), device_id_type=pl.DeviceIdType.MESH)
+
+        @pl.when(jnp.logical_and(j + 2 < nkb, jnp.logical_not(from_partner(j + 2))))
+        def _():
+            prefetch(j + 2)
+
         step(2 * j, s00, s01, s10, s11, c01, c00, c11, c10, False)
-
-        @pl.when(jnp.logical_and(from_partner(j - 1), j - 1 < nkb - parts))
-        def _():
-            pl.semaphore_signal(free.at[part_of(j - 1)], inc=1, device_id=(partner,), device_id_type=pl.DeviceIdType.MESH)
-
-        @pl.when(jnp.logical_and(j + 2 < nkb, jnp.logical_not(from_partner(j + 2))))
-        def _():
-            prefetch(j + 2)
-
         step(2 * j + 1, s01, s00, s11, s10, c00, c01, c10, c11, False)
         return 0
 
@@ -319,7 +317,7 @@
 
     lax.fori_loop(parts, chips * parts, drain_hops, 0)
     lax.fori_loop(0, parts, drain_first, 0)
-    lax.fori_loop(1, parts, drain_last, 0)
+    lax.fori_loop(0, parts, drain_last, 0)
 
 
 def both_sides(coef, img, txt, n_dev):
@@ -334,10 +332,10 @@
         out_shape=(grad, grad, jax.ShapeDtypeStruct((3, 8, 128), jnp.float32), whole, whole),
         in_specs=[pl.BlockSpec(memory_space=pltpu.SMEM), in_vmem, in_vmem, anywhere, anywhere],
         out_specs=(in_vmem, in_vmem, in_vmem, anywhere, anywhere),
-        scratch_shapes=[pltpu.VMEM((3 + rows // BK, BK, depth), jnp.bfloat16)] * 2
+        scratch_shapes=[pltpu.VMEM((2 * (rows // BK), BK, depth), jnp.bfloat16)] * 2
         + [pltpu.VMEM((BQ, BK), jnp.float32)] * 4
         + [pltpu.VMEM((BQ, BK), jnp.bfloat16)] * 4
-        + [pltpu.SemaphoreType.DMA((2, 3))]
+        + [pltpu.SemaphoreType.DMA((2, rows // BK))]
         + [pltpu.SemaphoreType.DMA((messages,))] * 4
         + [pltpu.VMEM((3, 8, 128), jnp.float32), pltpu.VMEM((n_dev, 3, 8, 128), jnp.float32)]
         + [pltpu.SemaphoreType.DMA((n_dev,))] * 2

time: 732 us -> 545 us (0.74)
  Pallas kernels: 712 us -> 525 us
    pallas_call x1, Pallas kernels: 712 us -> 525 us  [both_sides(): pl.pallas_call(kernel, out_shape=(grad, grad, jax.ShapeDtypeStruct((3, 8,...]
where the time goes in v3:
time: 545 us; the launch traced here: 544 us
  Pallas kernels  525 us (96%)
  other arithmetic  11.6 us (2%)
  between operations  7.31 us (1%)
    pallas_call x1, Pallas kernels, both_sides(): pl.pallas_call(kernel, out_shape=(grad, grad, jax.ShapeDtypeStruct((3, 8,...  525 us

profile of v3, /device:TPU:0, one launch (start us, length us, event | category | flops | bytes accessed | tf_op | source)
XLA Modules:
  0.0 544.4 jit_solution(3187458479625858519)
XLA Ops:
  2.0 0.6 pad_maximum_fusion.coef
  2.6 525.0 %shard_map.83 = (f32[2048,768]{1,0:T(8,128)}, f32[2048,768]{1,0:T(8,128)}, f32[3,8,128]{2,1,0:T(8,128)}, bf16[16384,768]{1,0:T(8,128)(2,1)}, bf16[16384,768]{1,0:T(8,128)(2,1)}) custom-call(f32[2]{0:T(128)} %pad_maximum_fusion.coef, bf16[2048,768]{1,0:T(8,128)(2,1)} %own1_ref.1, bf16[2048,768]{1,0:T(8,128)(2,1)} %own0_ref.1, bf16[2048,768]{1,0:T(8,128)(2,1)} %own0_ref.1, ...), custom_call_target="tpu_custom_call" | custom-call | tf_op jit(solution)/shard_map/pallas_call | solution.py:330
  527.5 0.8 reduce_sum.9
  528.3 0.6 fusion
  530.9 10.2 %broadcast_multiply_fusion = (f32[2048,768]{1,0:T(8,128)}, f32[2048,768]{1,0:T(8,128)}) fusion(f32[2048,768]{1,0:T(8,128)} %get-tuple-element.10, f32[]{:T(128)} %bitcast, f32[2048,768]{1,0:T(8,128)} %get-tuple-element.9), kind=kLoop, calls=%fused_computation | loop fusion | flops 3145728 | bytes 25165828 | tf_op jit(solution)/shard_map/mul | solution.py:358
